TPU v7x, 32 devices: a whole 2x2x4 slice. The times are simulated.
32 devices in a mesh: freq: 4 (over y, core), lat: 8 (over z, x).
Axes of the slice: x: 2, y: 2, z: 4, core: 2. Of those that a mesh axis runs over, the one named last changes fastest.
Arguments:
- spectra: float32 [2, 4, 32768], P(None, None, ('freq', 'lat')), may hold values from -6 to 6
- tile_route: int32 [32768, 1], P(('freq', 'lat')), may hold values from 0 to 255; in each aligned block of 1024 rows (0 to 1023, 1024 to 2047, ...) at most 8 rows name the same one
- bin_in_tile: int32 [32768], P(('freq', 'lat')), may hold values from 0 to 1023
- trace_offset: float32 [2, 32768], P(None, ('freq', 'lat')), may hold values from -0.5 to 0.5
- weights: float32 [32768], P(('freq', 'lat')), may hold values from 0.2 to 5
- frequency: float32 [4], P('freq'), may hold values from 0.5 to 1.5
- slowness: float32 [2, 8], replicated, may hold values from 0.6 to 1.6
- vel_index: int32 [2, 512, 512], P(None, 'lat'), may hold values from 0 to 7
Outputs:
- wavefield: float32 [2, 4, 512, 512], P(None, 'freq', 'lat')
- depth_image: float32 [2, 512, 512], P(None, 'lat', 'freq')
Inputs may be any that keep to these rules, and one draw needn't show every extreme that they name: `tile_route`: tiles of 32 x 32 bins, numbered row by row over the grid; among the rows of one device no tile is named by more than 8 traces. `bin_in_tile`: row * 32 + column of the bin within the tile.
All inputs are finite; a program needn't handle non-finite values.
Results may differ from a plain program's by a relative error of at most 0.0003.
Values sent between devices are 32-bit elements; how exact they have to be, the bound alone decides.
A program may use at most 64 MiB of HBM per device.

v0:
```python
import math
import jax
import jax.numpy as jnp
from jax import lax
from jax.sharding import PartitionSpec as P

NX = 512
NY = 512
TB = 32
MODES = 8
NSTEPS = 2
NREF = 2
NVEL = 8
TILES = 256
CAP = 8
damping = 1.0
depth_step = 1.0
block_tiles = 8


def dft_real(length, direction):
    counter = jnp.arange(length)
    angles = (
        2.0 * math.pi / length * (counter[:, None] * counter[None, :] % length).astype(jnp.float32)
    )
    cosine = jnp.cos(angles)
    sine_part = direction * jnp.sin(angles)
    return jnp.stack([jnp.stack([cosine, sine_part], 1), jnp.stack([-sine_part, cosine], 1)], 0)


def twiddle(full_length, first_len, second_len, direction):
    first_at = jnp.arange(first_len)[:, None]
    second_at = jnp.arange(second_len)[None, :]
    angles = 2.0 * math.pi / full_length * (first_at * second_at % full_length).astype(jnp.float32)
    return (jnp.cos(angles), direction * jnp.sin(angles))


def complex_scale(values, cosine, sine_part, part_axis):
    real_part = jnp.take(values, 0, axis=part_axis)
    imag_part = jnp.take(values, 1, axis=part_axis)
    return jnp.stack(
        [real_part * cosine - imag_part * sine_part, real_part * sine_part + imag_part * cosine],
        part_axis,
    )


def normal_terms(trace_meta, values_in):
    slot_count = trace_meta.shape[-1]
    tile_count = slot_count // CAP
    block_width = block_tiles * CAP
    mode_ids = jnp.arange(MODES).astype(jnp.float32)[:, None, None, None, None]

    def one_block(block_at):
        meta_part = lax.dynamic_slice_in_dim(trace_meta, block_at * block_width, block_width, 4)
        data_part = lax.dynamic_slice_in_dim(values_in, block_at * block_width, block_width, 4)
        meta_part = meta_part.reshape(meta_part.shape[:4] + (block_tiles, CAP))
        data_part = data_part.reshape(data_part.shape[:4] + (block_tiles, CAP))
        weight_part = meta_part[0, :, 0]
        along_x = jnp.cos(math.pi * mode_ids * (meta_part[1, :, 0][None] + 0.5) / TB)
        along_y = jnp.cos(math.pi * mode_ids * (meta_part[2, :, 0][None] + 0.5) / TB)
        basis_vals = (along_x[:, None] * along_y[None, :]).reshape(
            (MODES * MODES,) + weight_part.shape
        )
        weighted = basis_vals * weight_part[None]
        normal = jnp.einsum(
            "iabgc,jabgc->gij", weighted, basis_vals, precision=lax.Precision.HIGHEST
        )
        right_side = jnp.einsum(
            "iabgc,paqbgc->gipq", weighted, data_part, precision=lax.Precision.HIGHEST
        )
        return (normal, right_side)

    normal, right_side = lax.map(one_block, jnp.arange(tile_count // block_tiles))
    normal = normal.reshape(tile_count, MODES * MODES, MODES * MODES)
    right_side = right_side.reshape((tile_count, MODES * MODES) + right_side.shape[3:])
    return (normal, right_side)


def fit_grid(normal, right_side, row_count):
    tile_count = normal.shape[0]
    system = normal + damping * jnp.eye(MODES * MODES, dtype=jnp.float32)
    factor = jnp.linalg.cholesky(system)
    flat_rhs = right_side.reshape(tile_count, MODES * MODES, -1)
    middle = jax.scipy.linalg.solve_triangular(factor, flat_rhs, lower=True)
    coeffs = jax.scipy.linalg.solve_triangular(factor, middle, lower=True, trans="T")
    coeffs = coeffs.reshape(row_count // TB, NY // TB, MODES, MODES, 2, -1)
    cell_pos = jnp.arange(TB).astype(jnp.float32)
    cos_table = jnp.cos(
        math.pi * jnp.arange(MODES).astype(jnp.float32)[:, None] * (cell_pos[None, :] + 0.5) / TB
    )
    viewed = jnp.einsum(
        "xyabpq,ai,bj->pqxiyj", coeffs, cos_table, cos_table, precision=lax.Precision.HIGHEST
    )
    return viewed.reshape(2, viewed.shape[1], row_count, NY)


def local(spectra, tile_route, bin_in_tile, trace_offset, weights, frequency, slowness, vel_index):
    lat_count = lax.axis_size("lat")
    row_count = vel_index.shape[1]
    tile_dev = TILES // lat_count
    slot_count = tile_dev * CAP
    total_freqs = spectra.shape[1]
    tile_id = tile_route[:, 0]
    trace_count = tile_id.shape[0]
    ranking = jnp.argsort(tile_id, stable=True)
    sorted_tiles = tile_id[ranking]
    firsts = jnp.searchsorted(sorted_tiles, sorted_tiles, side="left")
    position = sorted_tiles * CAP + jnp.arange(trace_count, dtype=jnp.int32) - firsts
    slot_of = jnp.zeros((trace_count,), jnp.int32).at[ranking].set(position)
    owner_lat = slot_of // slot_count
    within = slot_of % slot_count
    cell_x = (bin_in_tile // TB).astype(jnp.float32) + trace_offset[0]
    cell_y = (bin_in_tile % TB).astype(jnp.float32) + trace_offset[1]
    trace_meta = jnp.stack([weights, cell_x, cell_y], 0)
    meta_buf = (
        jnp.zeros((3, lat_count, slot_count), jnp.float32).at[:, owner_lat, within].set(trace_meta)
    )
    spec_buf = (
        jnp.zeros((2, total_freqs, lat_count, slot_count), jnp.float32)
        .at[:, :, owner_lat, within]
        .set(spectra)
    )
    got_spec, got_meta = (
        lax.all_to_all(spec_buf, "lat", split_axis=2, concat_axis=2, tiled=True),
        lax.all_to_all(meta_buf[:, None], "lat", split_axis=2, concat_axis=2, tiled=True),
    )
    normal, right_side = normal_terms(got_meta[:, None], got_spec[:, None])
    normal = lax.psum(normal, "freq")
    right_side = lax.psum_scatter(right_side, "freq", scatter_dimension=3, tiled=True)
    wave_field = fit_grid(normal, right_side, row_count)
    len_x = NX // 8
    len_y = NY // 8
    w8_fwd = dft_real(8, -1.0)
    w8_inv = dft_real(8, 1.0)
    wx_fwd = dft_real(len_x, -1.0)
    wx_inv = dft_real(len_x, 1.0)
    wy_fwd = dft_real(len_y, -1.0)
    wy_inv = dft_real(len_y, 1.0)
    twx_fwd = twiddle(NX, 8, len_x, -1.0)
    twx_inv = twiddle(NX, 8, len_x, 1.0)
    twy_fwd = twiddle(NY, 8, len_y, -1.0)
    twy_inv = twiddle(NY, 8, len_y, 1.0)
    inverse_scale = 1.0 / (NX * NY)

    def forward_x(columns):
        dims_of = columns.shape
        viewed = columns.reshape(dims_of[:4] + (8, len_x))
        section_a = jnp.einsum(
            "phkqmn,pmsl->shkqln", viewed, w8_fwd, precision=lax.Precision.HIGHEST
        )
        section_b = complex_scale(section_a, twx_fwd[0], twx_fwd[1], 0)
        return jnp.einsum("shkqln,snto->thkqlo", section_b, wx_fwd, precision=lax.Precision.HIGHEST)

    def inverse_y(columns):
        section_c = jnp.einsum(
            "jthkqr,thsn->jsqrkn", columns, wy_inv, precision=lax.Precision.HIGHEST
        )
        section_b = complex_scale(section_c, twy_inv[0], twy_inv[1], 1)
        section_a = jnp.einsum(
            "jsqrkn,skpm->jpqrmn", section_b, w8_inv, precision=lax.Precision.HIGHEST
        )
        return section_a.reshape(section_a.shape[:4] + (NY,)) * inverse_scale

    lat_at = lax.axis_index("lat")
    ky_band = len_y // lat_count
    ky_index = jnp.arange(8)[None, :] + 8 * (lat_at * ky_band + jnp.arange(ky_band)[:, None])
    ky_signed = jnp.where(ky_index >= NY // 2, ky_index - NY, ky_index)
    ky_vals = 2.0 * math.pi / NY * ky_signed.astype(jnp.float32)
    kx_index = jnp.arange(8)[:, None] + 8 * jnp.arange(len_x)[None, :]
    kx_signed = jnp.where(kx_index >= NX // 2, kx_index - NX, kx_index)
    kx_vals = 2.0 * math.pi / NX * kx_signed.astype(jnp.float32)
    ky_sq = (ky_vals * ky_vals)[None, :, :, None, None, None]
    kx_sq = (kx_vals * kx_vals)[None, None, None, None, :, :]
    per_group = NVEL // NREF
    image_rows = []
    for depth_at in range(NSTEPS):
        table_row = slowness[depth_at]
        references = table_row.reshape(NREF, per_group).mean(axis=1)
        forward_dims_of = wave_field.shape
        forward_viewed = wave_field.reshape(forward_dims_of[:3] + (8, len_y))
        forward_section_a = jnp.einsum(
            "pqrmn,pmsk->sqrkn", forward_viewed, w8_fwd, precision=lax.Precision.HIGHEST
        )
        forward_section_b = complex_scale(forward_section_a, twy_fwd[0], twy_fwd[1], 0)
        spectrum_y = jnp.einsum(
            "sqrkn,snth->thkqr", forward_section_b, wy_fwd, precision=lax.Precision.HIGHEST
        )
        spectrum = forward_x(
            lax.all_to_all(spectrum_y, "lat", split_axis=1, concat_axis=4, tiled=True)
        )
        wave_num = frequency[None, :] * references[:, None]
        vertical = (wave_num * wave_num)[:, None, None, :, None, None] - kx_sq - ky_sq
        phase_angle = jnp.sqrt(jnp.maximum(vertical, 0.0)) * depth_step
        damped = jnp.exp(-jnp.sqrt(jnp.maximum(-vertical, 0.0)) * depth_step)
        shifted = complex_scale(
            spectrum[None], damped * jnp.cos(phase_angle), damped * jnp.sin(phase_angle), 1
        )
        inverse_section_c = jnp.einsum(
            "jthkqlo,tosn->jshkqln", shifted, wx_inv, precision=lax.Precision.HIGHEST
        )
        inverse_section_b = complex_scale(inverse_section_c, twx_inv[0], twx_inv[1], 1)
        inverse_section_a = jnp.einsum(
            "jshkqln,slpm->jphkqmn", inverse_section_b, w8_inv, precision=lax.Precision.HIGHEST
        )
        columns = inverse_section_a.reshape(inverse_section_a.shape[:5] + (NX,))
        returned = inverse_y(
            lax.all_to_all(columns, "lat", split_axis=5, concat_axis=2, tiled=True)
        )
        velocity = vel_index[depth_at]
        picked = velocity[None] == jnp.arange(NVEL)[:, None, None]
        local_slow = jnp.sum(jnp.where(picked, table_row[:, None, None], 0.0), 0)
        group_of = velocity // per_group
        split_phase = (
            frequency[None, :, None, None]
            * (local_slow[None, None] - references[:, None, None, None])
            * depth_step
        )
        group_mask = (group_of[None] == jnp.arange(NREF)[:, None, None]).astype(jnp.float32)
        corrected = complex_scale(returned, jnp.cos(split_phase), jnp.sin(split_phase), 1)
        wave_field = jnp.sum(corrected * group_mask[:, None, None], 0)
        summed = jnp.sum(wave_field[0], 0)
        image_rows.append(lax.psum_scatter(summed, "freq", scatter_dimension=1, tiled=True))
    depth_image = jnp.stack(image_rows, 0)
    return (wave_field, depth_image)


def solution(mesh):
    return jax.shard_map(
        local,
        mesh=mesh,
        in_specs=(
            P(None, None, ("freq", "lat")),
            P(("freq", "lat"), None),
            P(("freq", "lat")),
            P(None, ("freq", "lat")),
            P(("freq", "lat")),
            P("freq"),
            P(),
            P(None, "lat", None),
        ),
        out_specs=(P(None, "freq", "lat", None), P(None, "lat", "freq")),
        check_vma=False,
    )
```

profile of v0, /device:TPU:0, one launch (start us, length us, event | category | flops | bytes accessed | tf_op | source)
XLA Modules:
  0.0 646.6 jit_solution(14288893780096186821)
XLA Ops:
  7.2 5.1 sort.17
  16.9 50.7 %while.52 = (s32[]{:T(128)}, u32[1024]{0:T(1024)S(1)}, u32[1024]{0:T(1024)S(1)}, s32[1024]{0:T(1024)S(1)}, s32[]{:T(128)}, /*index=5*/s32[]{:T(128)}, s32[]{}) while((s32[]{:T(128)}, u32[1024]{0:T(1024)S(1)}, u32[1024]{0:T(1024)S(1)}, s32[1024]{0:T(1024)S(1)}, s32[]{:T(128)}, /*index=5*/s32[]{:T(128)}, s32[]{}) %tuple.186), condition=%wide.region_2.3_spmd.clone, body=%wide.region_1.2_spmd.clone.sunk | while | flops 19460 | bytes 67685 | solution.py:107
  76.8 7.3 %all-to-all-start = ((f32[3,1,8,256]{3,1,0,2:T(1,128)}), f32[3,1,8,256]{3,1,0,2:T(1,128)S(1)}, u32[]{:S(2)}, u32[]{:S(2)}) async-start(f32[3,1,8,256]{3,1,0,2:T(1,128)} %copy.348), calls=%async_computation | async-start | bytes 49152 | tf_op jit(solution)/shard_map/all_to_all | solution.py:125
  93.0 26.6 %scatter_fusion = f32[2,4,2048]{1,0,2:T(2,128)S(1)} fusion(f32[2,4,2048]{1,0,2:T(2,128)S(1)} %broadcast.1405, s32[1024]{0:T(1024)S(1)} %broadcast_select_fusion, f32[1024,2,4]{2,1,0:T(2,128)S(1)} %copy.350), kind=kCustom, calls=%fused_computation.4 | custom fusion | bytes 102400
  121.5 6.0 all-to-all-start.1
  129.2 5.2 all-to-all-done.1
  134.4 30.9 %while.51 = (s32[]{:T(128)}, f32[4,8,64,64]{2,3,1,0:T(8,128)}, f32[4,8,64,2,4]{2,1,0,3,4:T(8,128)}, s32[4]{0:T(128)S(1)}, f32[3,1,1,8,256]{4,3,2,1,0:T(8,128)S(1...) while((s32[]{:T(128)}, f32[4,8,64,64]{2,3,1,0:T(8,128)}, ...), condition=%wide.region_7.8_spmd.clone.clone, body=%wide.region_6.7_spmd.clone.clone.sunk | while | flops 28427288 | bytes 1600791 | solution.py:73
  167.1 32.2 %all-reduce.2.cloned.1.call-done = f32[32,64,64]{1,2,0:T(8,128)} async-done(((f32[32,64,64]{1,2,0:T(8,128)}), f32[32,64,64]{1,2,0:T(8,128)}) %all-reduce.2.cloned.1.call-update) | async-done | bytes 524304 | tf_op jit(solution)/shard_map/psum | solution.py:128
  202.1 188.3 %custom-call.11 = f32[32,64,64]{2,1,0:T(8,128)} custom-call(f32[32,64,64]{2,1,0:T(8,128)S(1)} %fusion.24), custom_call_target="Cholesky" | custom-call | tf_op jit(solution)/shard_map/jit(cholesky)/cholesky | solution.py:82
  394.8 67.2 %custom-call.12 = f32[32,1,64,64]{0,2,3,1:T(8,128)S(1)} custom-call(f32[32,1,64,64]{0,3,2,1:T(8,128)} %select_bitcast_fusion), custom_call_target="InvertDiagBlocksLowerTriangular" | custom-call | tf_op jit(solution)/shard_map/jit(_solve_triangular)/vmap()/triangular_solve | solution.py:85
  473.8 5.9 all-to-all-start.2
  480.7 7.5 %all-to-all-done.2 = f32[8,1,8192]{2,1,0:T(1,128)S(1)} async-done(((f32[8,1,8192]{2,1,0:T(1,128)}), f32[8,1,8192]{2,1,0:T(1,128)S(1)}, u32[]{:S(2)}, u32[]{:S(2)}) %all-to-all-start.2) | async-done | bytes 262176 | tf_op jit(solution)/shard_map/all_to_all | solution.py:189
  496.5 4.9 copy.445
  501.4 7.3 %reshape.1555 = f32[8,1,16384]{2,1,0:T(1,128)} reshape(f32[512,1,2,2,8,8]{5,4,3,2,1,0:T(8,128)} %bitcast.594) | data formatting | bytes 1048576
  513.7 12.8 %all-to-all-done.3 = f32[8,1,16384]{2,1,0:T(1,128)S(1)} async-done(((f32[8,1,16384]{2,1,0:T(1,128)}), f32[8,1,16384]{2,1,0:T(1,128)S(1)}, u32[]{:S(2)}, u32[]{:S(2)}) %all-to-all-start.3) | async-done | bytes 524320 | tf_op jit(solution)/shard_map/all_to_all | solution.py:207
  528.4 7.8 %reshape.1556 = f32[512,1,2,2,8,8]{5,4,3,2,1,0:T(8,128)} reshape(f32[8,16384]{1,0:T(8,128)S(1)} %reduce.23) | data formatting | bytes 1048576
  536.2 5.4 copy.379
  548.8 12.5 %all_to_all.70 = f32[8,1,8192]{2,1,0:T(1,128)S(1)} all-to-all(f32[8,1,8192]{2,1,0:T(1,128)S(1)} %reshape.1557), channel_id=1, replica_groups=mesh['freq'=4,'lat'=8] {'lat'}, dimensions={0} | all-to-all | bytes 524288 | tf_op jit(solution)/shard_map/all_to_all | solution.py:189
  569.0 4.9 copy.448
  573.9 7.3 %reshape.1559 = f32[8,1,16384]{2,1,0:T(1,128)} reshape(f32[512,1,2,2,8,8]{5,4,3,2,1,0:T(8,128)} %bitcast.596) | data formatting | bytes 1048576
  585.8 13.1 %all-to-all-done.5 = f32[8,1,16384]{2,1,0:T(1,128)S(1)} async-done(((f32[8,1,16384]{2,1,0:T(1,128)}), f32[8,1,16384]{2,1,0:T(1,128)S(1)}, u32[]{:S(2)}, u32[]{:S(2)}) %all-to-all-start.5) | async-done | bytes 524320 | tf_op jit(solution)/shard_map/all_to_all | solution.py:207
  600.9 7.8 %reshape.1560 = f32[512,1,2,2,8,8]{5,4,3,2,1,0:T(8,128)} reshape(f32[8,16384]{1,0:T(8,128)S(1)} %reduce.25) | data formatting | bytes 1048576
  608.7 5.4 copy.394
  619.4 18.9 %reduce-scatter.8.cloned.1.call-done = f32[64,128]{1,0:T(8,128)} async-done(((f32[64,512]{1,0:T(8,128)}), f32[64,128]{1,0:T(8,128)}) %reduce-scatter.8.cloned.1.call-update) | async-done | bytes 32784 | tf_op jit(solution)/shard_map/reduce_scatter | solution.py:222
  (351 shorter events, 167.4 us)
Async XLA Ops:
  16.8 55.2 %copy-start.41 = (s32[2]{0:T(128)S(1)}, s32[2]{0:T(128)}, u32[]{:S(2)}) copy-start(s32[2]{0:T(128)} %constant.465) | copy-start | bytes 28
  16.9 55.3 %copy-start.40 = (s32[2]{0:T(128)S(1)}, s32[2]{0:T(128)}, u32[]{:S(2)}) copy-start(s32[2]{0:T(128)} %constant.468) | copy-start | bytes 28
  16.9 55.4 %copy-start.28 = (f32[2,1024]{1,0:T(2,128)S(1)}, f32[2,1024]{1,0:T(2,128)}, u32[]{:S(2)}) copy-start(f32[2,1024]{1,0:T(2,128)} %param.39) | copy-start | bytes 24580
  16.9 55.4 %copy-start.29 = (s32[1024]{0:T(1024)S(1)}, s32[1024]{0:T(1024)}, u32[]{:S(2)}) copy-start(s32[1024]{0:T(1024)} %param.38) | copy-start | bytes 12292
  16.9 55.4 %copy-start.30 = (f32[1024]{0:T(1024)S(1)}, f32[1024]{0:T(1024)}, u32[]{:S(2)}) copy-start(f32[1024]{0:T(1024)} %param.40) | copy-start | bytes 12292
  67.6 20.1 %copy-start.39 = (f32[2,8]{1,0:T(2,128)S(1)}, f32[2,8]{1,0:T(2,128)}, u32[]{:S(2)}) copy-start(f32[2,8]{1,0:T(2,128)} %param.42) | copy-start | bytes 196
  67.7 24.2 %copy-start.22 = (f32[2,4,1024]{2,1,0:T(4,128)S(1)}, f32[2,4,1024]{2,1,0:T(4,128)}, u32[]{:S(2)}) copy-start(f32[2,4,1024]{2,1,0:T(4,128)} %param.36) | copy-start | bytes 98308
  76.8 44.7 %all-to-all-start = ((f32[3,1,8,256]{3,1,0,2:T(1,128)}), f32[3,1,8,256]{3,1,0,2:T(1,128)S(1)}, u32[]{:S(2)}, u32[]{:S(2)}) async-start(f32[3,1,8,256]{3,1,0,2:T(1,128)} %copy.348), calls=%async_computation | async-start | bytes 49152 | tf_op jit(solution)/shard_map/all_to_all | solution.py:125
  121.5 12.9 %all-to-all-start.1 = ((f32[2,4,8,256]{3,1,0,2:T(4,128)}), f32[2,4,8,256]{3,1,0,2:T(4,128)S(1)}, u32[]{:S(2)}, u32[]{:S(2)}) async-start(f32[2,4,8,256]{3,1,0,2:T(4,128)} %copy.351), calls=%async_computation.1 | async-start | bytes 131072 | tf_op jit(solution)/shard_map/all_to_all | solution.py:124
  127.5 71.8 %all-reduce.2.cloned.1.call-start = ((), (), s32[]{:S(2)}) async-start(), calls=%async_computation.9 | async-start | bytes 2097152 | tf_op jit(solution)/shard_map/psum | solution.py:128
  134.4 31.2 %copy-start.13 = (f32[64,64]{1,0:T(8,128)S(1)}, f32[64,64]{1,0:T(8,128)}, u32[]{:S(2)}) copy-start(f32[64,64]{1,0:T(8,128)} %fusion.111) | copy-start | bytes 49156
  134.4 31.3 %copy-start.26 = (f32[1,8,2,8]{3,1,2,0:T(8,128)S(1)}, f32[1,8,2,8]{3,1,2,0:T(8,128)}, u32[]{:S(2)}) copy-start(f32[1,8,2,8]{3,1,2,0:T(8,128)} %get-tuple-element.409) | copy-start | bytes 1540
  134.4 31.4 %copy-start.25 = (f32[1,8,2,8]{3,1,2,0:T(8,128)S(1)}, f32[1,8,2,8]{3,1,2,0:T(8,128)}, u32[]{:S(2)}) copy-start(f32[1,8,2,8]{3,1,2,0:T(8,128)} %get-tuple-element.408) | copy-start | bytes 1540
  165.4 298.2 %reduce-scatter.4.cloned.1.call-start = ((), (), s32[]{:S(2)}) async-start(), calls=%async_computation.10 | async-start | bytes 163840 | tf_op jit(solution)/shard_map/reduce_scatter | solution.py:129
  165.7 33.6 %copy-start.5 = (f32[64,64]{0,1:T(8,128)}, f32[64,64]{0,1:T(8,128)S(1)}, u32[]{:S(2)}) copy-start(f32[64,64]{0,1:T(8,128)S(1)} %copy.355) | copy-start | bytes 49156
  473.8 14.4 %all-to-all-start.2 = ((f32[8,1,8192]{2,1,0:T(1,128)}), f32[8,1,8192]{2,1,0:T(1,128)S(1)}, u32[]{:S(2)}, u32[]{:S(2)}) async-start(f32[8,1,8192]{2,1,0:T(1,128)} %reshape.1553), calls=%async_computation.3 | async-start | bytes 524288 | tf_op jit(solution)/shard_map/all_to_all | solution.py:189
  479.9 15.6 %copy-start.9 = (f32[1,8,2,8]{1,3,0,2:T(8,128)}, f32[1,8,2,8]{1,3,0,2:T(8,128)S(1)}, u32[]{:S(2)}) copy-start(f32[1,8,2,8]{1,3,0,2:T(8,128)S(1)} %copy.342) | copy-start | bytes 1540
  479.9 15.5 %copy-start.11 = (f32[1,8,2,8]{1,3,0,2:T(8,128)}, f32[1,8,2,8]{1,3,0,2:T(8,128)S(1)}, u32[]{:S(2)}) copy-start(f32[1,8,2,8]{1,3,0,2:T(8,128)S(1)} %copy.343) | copy-start | bytes 1540
  480.0 11.9 %copy-start.17 = (f32[8,8]{1,0:T(8,128)}, f32[8,8]{1,0:T(8,128)S(1)}, u32[]{:S(2)}) copy-start(f32[8,8]{1,0:T(8,128)S(1)} %fusion.131) | copy-start | bytes 772
  508.8 17.7 %all-to-all-start.3 = ((f32[8,1,16384]{2,1,0:T(1,128)}), f32[8,1,16384]{2,1,0:T(1,128)S(1)}, u32[]{:S(2)}, u32[]{:S(2)}) async-start(f32[8,1,16384]{2,1,0:T(1,128)} %reshape.1555), calls=%async_computation.4 | async-start | bytes 1048576 | tf_op jit(solution)/shard_map/all_to_all | solution.py:207
  581.2 17.8 %all-to-all-start.5 = ((f32[8,1,16384]{2,1,0:T(1,128)}), f32[8,1,16384]{2,1,0:T(1,128)S(1)}, u32[]{:S(2)}, u32[]{:S(2)}) async-start(f32[8,1,16384]{2,1,0:T(1,128)} %reshape.1559), calls=%async_computation.6 | async-start | bytes 1048576 | tf_op jit(solution)/shard_map/all_to_all | solution.py:207
  584.8 34.6 %reduce-scatter.6.cloned.1.call-start = ((), (), s32[]{:S(2)}) async-start(), calls=%async_computation.11 | async-start | bytes 163840 | tf_op jit(solution)/shard_map/reduce_scatter | solution.py:222
  585.5 52.7 %reduce-scatter.8.cloned.1.call-start = ((), (), s32[]{:S(2)}) async-start(), calls=%async_computation.12 | async-start | bytes 163840 | tf_op jit(solution)/shard_map/reduce_scatter | solution.py:222
  618.6 21.0 %copy-start.2 = (f32[2,64,512]{2,1,0:T(8,128)}, f32[2,64,512]{2,1,0:T(8,128)S(1)}, u32[]{:S(2)}) copy-start(f32[2,64,512]{2,1,0:T(8,128)S(1)} %fusion.46) | copy-start | bytes 786436
  (27 other events, 117.4 us)
Sparse Core Ops, SparseCore 0:
  165.5 33.8 all-reduce.1
  202.3 20.4 reduce-scatter.3
  588.0 21.0 reduce-scatter.5
  619.5 18.7 reduce-scatter.7
where the time goes:
time: 656 us; the launch traced here: 647 us
  other arithmetic  302 us (46%)
  local copies, waits for them, and re-layouts  166 us (25%)
  waiting for transfers between devices  89.8 us (14%)
  matrix products  29.4 us (4%)
  starting transfers between devices  27.1 us (4%)
  between operations  16.1 us (2%)
  blocking collectives  12.5 us (2%)
    another operation x4, other arithmetic, fit_grid(): factor = jnp.linalg.cholesky(system)  190 us
    another operation x3, other arithmetic, fit_grid(): jax.scipy.linalg.solve_triangular(factor, middle, lower=True, trans='T')  69.5 us
    unnamed x96, local copies, waits for them, and re-layouts  63.4 us
    gather x11, local copies, waits for them, and re-layouts, local(): firsts = jnp.searchsorted(sorted_tiles, sorted_tiles, side='left')  49.8 us
    psum x1, waiting for transfers between devices, local(): normal = lax.psum(normal, 'freq')  32.2 us
    all_to_all x2, waiting for transfers between devices, local(): lax.all_to_all(columns, 'lat', split_axis=5, concat_axis=2, tiled=True)  25.9 us
    reduce_scatter x2, waiting for transfers between devices, local(): lax.psum_scatter(summed, 'freq', scatter_dimension=1, tiled=True)  18.9 us
  transfers between devices with their start and end apart: 9, of which 6 were waited for; matrix products, arithmetic and copies ran while one was open for 51% of the time, Pallas kernels for 0%

commit v1 on v0

--- a/solution.py
+++ b/solution.py
@@ -203,9 +203,13 @@
             "jshkqln,slpm->jphkqmn", inverse_section_b, w8_inv, precision=lax.Precision.HIGHEST
         )
         columns = inverse_section_a.reshape(inverse_section_a.shape[:5] + (NX,))
-        returned = inverse_y(
-            lax.all_to_all(columns, "lat", split_axis=5, concat_axis=2, tiled=True)
-        )
+        form_column = lambda inputs: jnp.concatenate(
+            jax.lax.all_to_all(
+                jnp.stack(jnp.split(inputs, jax.lax.axis_size("lat"), 5)), "lat", 0, 0
+            ),
+            2,
+        )
+        returned = inverse_y(form_column(columns))
         velocity = vel_index[depth_at]
         picked = velocity[None] == jnp.arange(NVEL)[:, None, None]
         local_slow = jnp.sum(jnp.where(picked, table_row[:, None, None], 0.0), 0)

time: 656 us -> 616 us (0.939)
  local copies, waits for them, and re-layouts: 166 us -> 121 us
    unnamed x96 -> x116, local copies, waits for them, and re-layouts: 63.4 us -> 37.5 us
    all_to_all x2 -> x0, local copies, waits for them, and re-layouts: 10.8 us -> none  [local(): lax.all_to_all(columns, 'lat', split_axis=5, concat_axis=2, tiled=True)]
    reshape x2, local copies, waits for them, and re-layouts: 9.87 us -> 0.54 us  [local(): columns = inverse_section_a.reshape(inverse_section_a.shape[:5] + (NX,))]
  transfers between devices with their start and end apart: 9 -> 9, of which waited for: 6 -> 7; matrix products, arithmetic and copies ran while one was open for 51% -> 52% of each run, Pallas kernels for 0% -> 0%
where the time goes in v1:
time: 616 us; the launch traced here: 607 us
  other arithmetic  303 us (49%)
  local copies, waits for them, and re-layouts  121 us (20%)
  waiting for transfers between devices  94.5 us (15%)
  matrix products  30.4 us (5%)
  starting transfers between devices  27.1 us (4%)
  between operations  16.1 us (3%)
  blocking collectives  12.4 us (2%)
    another operation x4, other arithmetic, fit_grid(): factor = jnp.linalg.cholesky(system)  190 us
    another operation x3, other arithmetic, fit_grid(): jax.scipy.linalg.solve_triangular(factor, middle, lower=True, trans='T')  69.6 us
    gather x11, local copies, waits for them, and re-layouts, local(): firsts = jnp.searchsorted(sorted_tiles, sorted_tiles, side='left')  49.8 us
    unnamed x116, local copies, waits for them, and re-layouts  37.5 us
    psum x1, waiting for transfers between devices, local(): normal = lax.psum(normal, 'freq')  32.3 us
    all_to_all x2, waiting for transfers between devices, local(): jax.lax.all_to_all(jnp.stack(jnp.split(inputs, jax.lax.axis_size('lat'),...  25.1 us
    reduce_scatter x2, waiting for transfers between devices, local(): lax.psum_scatter(summed, 'freq', scatter_dimension=1, tiled=True)  24.3 us
    all_to_all x1, blocking collectives, local(): lax.all_to_all(spectrum_y, 'lat', split_axis=1, concat_axis=4, tiled=True)  12.4 us
  transfers between devices with their start and end apart: 9, of which 7 were waited for; matrix products, arithmetic and copies ran while one was open for 52% of the time, Pallas kernels for 0%

profile of v1, /device:TPU:0, one launch (start us, length us, event | category | flops | bytes accessed | tf_op | source)
XLA Modules:
  0.0 607.4 jit_solution(3074003097794449078)
XLA Ops:
  7.2 5.1 sort.17
  12.3 4.5 gather_fusion.1
  16.9 50.7 %while.52 = (s32[]{:T(128)}, u32[1024]{0:T(1024)S(1)}, u32[1024]{0:T(1024)S(1)}, s32[1024]{0:T(1024)S(1)}, s32[]{:T(128)}, /*index=5*/s32[]{:T(128)}, s32[]{}) while((s32[]{:T(128)}, u32[1024]{0:T(1024)S(1)}, u32[1024]{0:T(1024)S(1)}, s32[1024]{0:T(1024)S(1)}, s32[]{:T(128)}, /*index=5*/s32[]{:T(128)}, s32[]{}) %tuple.186), condition=%wide.region_2.3_spmd.clone, body=%wide.region_1.2_spmd.clone.sunk | while | flops 19460 | bytes 67685 | solution.py:107
  16.9 4.5 gather_fusion
  21.5 4.5 gather_fusion
  26.2 4.5 gather_fusion
  30.8 4.5 gather_fusion
  35.4 4.5 gather_fusion
  40.0 4.5 gather_fusion
  49.2 4.5 gather_fusion
  76.8 7.3 %all-to-all-start = ((f32[3,1,8,256]{3,1,0,2:T(1,128)}), f32[3,1,8,256]{3,1,0,2:T(1,128)S(1)}, u32[]{:S(2)}, u32[]{:S(2)}) async-start(f32[3,1,8,256]{3,1,0,2:T(1,128)} %copy.340), calls=%async_computation | async-start | bytes 49152 | tf_op jit(solution)/shard_map/all_to_all | solution.py:125
  93.0 26.6 %scatter_fusion = f32[2,4,2048]{1,0,2:T(2,128)S(1)} fusion(f32[2,4,2048]{1,0,2:T(2,128)S(1)} %broadcast.1405, s32[1024]{0:T(1024)S(1)} %broadcast_select_fusion, f32[1024,2,4]{2,1,0:T(2,128)S(1)} %copy.342), kind=kCustom, calls=%fused_computation.4 | custom fusion | bytes 102400
  121.5 6.0 all-to-all-start.1
  129.2 5.2 all-to-all-done.1
  134.4 31.0 %while.51 = (s32[]{:T(128)}, f32[4,8,64,64]{2,3,1,0:T(8,128)}, f32[4,8,64,2,4]{2,1,0,3,4:T(8,128)}, s32[4]{0:T(128)S(1)}, f32[3,1,1,8,256]{4,3,2,1,0:T(8,128)S(1...) while((s32[]{:T(128)}, f32[4,8,64,64]{2,3,1,0:T(8,128)}, ...), condition=%wide.region_7.8_spmd.clone.clone, body=%wide.region_6.7_spmd.clone.clone.sunk | while | flops 28427288 | bytes 1600791 | solution.py:73
  167.1 32.3 %all-reduce.2.cloned.1.call-done = f32[32,64,64]{1,2,0:T(8,128)} async-done(((f32[32,64,64]{1,2,0:T(8,128)}), f32[32,64,64]{1,2,0:T(8,128)}) %all-reduce.2.cloned.1.call-update) | async-done | bytes 524304 | tf_op jit(solution)/shard_map/psum | solution.py:128
  202.2 188.3 %custom-call.11 = f32[32,64,64]{2,1,0:T(8,128)} custom-call(f32[32,64,64]{2,1,0:T(8,128)S(1)} %fusion.24), custom_call_target="Cholesky" | custom-call | tf_op jit(solution)/shard_map/jit(cholesky)/cholesky | solution.py:82
  394.9 67.2 %custom-call.12 = f32[32,1,64,64]{0,2,3,1:T(8,128)S(1)} custom-call(f32[32,1,64,64]{0,3,2,1:T(8,128)} %select_bitcast_fusion), custom_call_target="InvertDiagBlocksLowerTriangular" | custom-call | tf_op jit(solution)/shard_map/jit(_solve_triangular)/vmap()/triangular_solve | solution.py:85
  474.0 5.8 all-to-all-start.2
  480.6 7.5 %all-to-all-done.2 = f32[8,1,8192]{2,1,0:T(1,128)S(1)} async-done(((f32[8,1,8192]{2,1,0:T(1,128)}), f32[8,1,8192]{2,1,0:T(1,128)S(1)}, u32[]{:S(2)}, u32[]{:S(2)}) %all-to-all-start.2) | async-done | bytes 262176 | tf_op jit(solution)/shard_map/all_to_all | solution.py:189
  504.7 12.0 %all-to-all-done.3 = f32[8,1,16384]{2,1,0:T(1,128)S(1)} async-done(((f32[8,1,16384]{2,1,0:T(1,128)}), f32[8,1,16384]{2,1,0:T(1,128)S(1)}, u32[]{:S(2)}, u32[]{:S(2)}) %all-to-all-start.3) | async-done | bytes 524320 | tf_op jit(solution)/shard_map/all_to_all | solution.py:207
  527.0 12.4 %all_to_all.50 = f32[8,1,8192]{2,1,0:T(1,128)S(1)} all-to-all(f32[8,1,8192]{2,1,0:T(1,128)S(1)} %reshape.1567), channel_id=1, replica_groups=mesh['freq'=4,'lat'=8] {'lat'}, dimensions={0} | all-to-all | bytes 524288 | tf_op jit(solution)/shard_map/all_to_all | solution.py:189
  554.0 13.2 %all-to-all-done.5 = f32[8,1,16384]{2,1,0:T(1,128)S(1)} async-done(((f32[8,1,16384]{2,1,0:T(1,128)}), f32[8,1,16384]{2,1,0:T(1,128)S(1)}, u32[]{:S(2)}, u32[]{:S(2)}) %all-to-all-start.5) | async-done | bytes 524320 | tf_op jit(solution)/shard_map/all_to_all | solution.py:207
  577.3 21.9 %reduce-scatter.8.cloned.1.call-done = f32[64,128]{1,0:T(8,128)} async-done(((f32[64,512]{1,0:T(8,128)}), f32[64,128]{1,0:T(8,128)}) %reduce-scatter.8.cloned.1.call-update) | async-done | bytes 32784 | tf_op jit(solution)/shard_map/reduce_scatter | solution.py:226
  (373 shorter events, 140.8 us)
Async XLA Ops:
  16.8 55.2 %copy-start.44 = (s32[2]{0:T(128)S(1)}, s32[2]{0:T(128)}, u32[]{:S(2)}) copy-start(s32[2]{0:T(128)} %constant.465) | copy-start | bytes 28
  16.9 55.3 %copy-start.43 = (s32[2]{0:T(128)S(1)}, s32[2]{0:T(128)}, u32[]{:S(2)}) copy-start(s32[2]{0:T(128)} %constant.468) | copy-start | bytes 28
  16.9 55.4 %copy-start.31 = (f32[2,1024]{1,0:T(2,128)S(1)}, f32[2,1024]{1,0:T(2,128)}, u32[]{:S(2)}) copy-start(f32[2,1024]{1,0:T(2,128)} %param.39) | copy-start | bytes 24580
  16.9 55.4 %copy-start.32 = (s32[1024]{0:T(1024)S(1)}, s32[1024]{0:T(1024)}, u32[]{:S(2)}) copy-start(s32[1024]{0:T(1024)} %param.38) | copy-start | bytes 12292
  16.9 55.4 %copy-start.33 = (f32[1024]{0:T(1024)S(1)}, f32[1024]{0:T(1024)}, u32[]{:S(2)}) copy-start(f32[1024]{0:T(1024)} %param.40) | copy-start | bytes 12292
  67.6 20.2 %copy-start.42 = (f32[2,8]{1,0:T(2,128)S(1)}, f32[2,8]{1,0:T(2,128)}, u32[]{:S(2)}) copy-start(f32[2,8]{1,0:T(2,128)} %param.42) | copy-start | bytes 196
  67.7 24.2 %copy-start.25 = (f32[2,4,1024]{2,1,0:T(4,128)S(1)}, f32[2,4,1024]{2,1,0:T(4,128)}, u32[]{:S(2)}) copy-start(f32[2,4,1024]{2,1,0:T(4,128)} %param.36) | copy-start | bytes 98308
  76.8 44.6 %all-to-all-start = ((f32[3,1,8,256]{3,1,0,2:T(1,128)}), f32[3,1,8,256]{3,1,0,2:T(1,128)S(1)}, u32[]{:S(2)}, u32[]{:S(2)}) async-start(f32[3,1,8,256]{3,1,0,2:T(1,128)} %copy.340), calls=%async_computation | async-start | bytes 49152 | tf_op jit(solution)/shard_map/all_to_all | solution.py:125
  121.5 12.9 %all-to-all-start.1 = ((f32[2,4,8,256]{3,1,0,2:T(4,128)}), f32[2,4,8,256]{3,1,0,2:T(4,128)S(1)}, u32[]{:S(2)}, u32[]{:S(2)}) async-start(f32[2,4,8,256]{3,1,0,2:T(4,128)} %copy.343), calls=%async_computation.1 | async-start | bytes 131072 | tf_op jit(solution)/shard_map/all_to_all | solution.py:124
  127.5 72.0 %all-reduce.2.cloned.1.call-start = ((), (), s32[]{:S(2)}) async-start(), calls=%async_computation.9 | async-start | bytes 2097152 | tf_op jit(solution)/shard_map/psum | solution.py:128
  134.4 31.3 %copy-start.16 = (f32[64,64]{1,0:T(8,128)S(1)}, f32[64,64]{1,0:T(8,128)}, u32[]{:S(2)}) copy-start(f32[64,64]{1,0:T(8,128)} %fusion.129) | copy-start | bytes 49156
  134.4 31.3 %copy-start.29 = (f32[1,8,2,8]{3,1,2,0:T(8,128)S(1)}, f32[1,8,2,8]{3,1,2,0:T(8,128)}, u32[]{:S(2)}) copy-start(f32[1,8,2,8]{3,1,2,0:T(8,128)} %get-tuple-element.409) | copy-start | bytes 1540
  134.4 31.4 %copy-start.28 = (f32[1,8,2,8]{3,1,2,0:T(8,128)S(1)}, f32[1,8,2,8]{3,1,2,0:T(8,128)}, u32[]{:S(2)}) copy-start(f32[1,8,2,8]{3,1,2,0:T(8,128)} %get-tuple-element.408) | copy-start | bytes 1540
  165.4 298.3 %reduce-scatter.4.cloned.1.call-start = ((), (), s32[]{:S(2)}) async-start(), calls=%async_computation.10 | async-start | bytes 163840 | tf_op jit(solution)/shard_map/reduce_scatter | solution.py:129
  165.7 33.7 %copy-start.7 = (f32[64,64]{0,1:T(8,128)}, f32[64,64]{0,1:T(8,128)S(1)}, u32[]{:S(2)}) copy-start(f32[64,64]{0,1:T(8,128)S(1)} %copy.347) | copy-start | bytes 49156
  165.8 305.0 %copy-start.11 = (f32[1,8,2,8]{1,3,0,2:T(8,128)}, f32[1,8,2,8]{1,3,0,2:T(8,128)S(1)}, u32[]{:S(2)}) copy-start(f32[1,8,2,8]{1,3,0,2:T(8,128)S(1)} %copy.337) | copy-start | bytes 1540
  472.6 17.6 %copy-start.12 = (f32[1,8,2,8]{1,3,0,2:T(8,128)S(1)}, f32[1,8,2,8]{1,3,0,2:T(8,128)}, u32[]{:S(2)}) copy-start(f32[1,8,2,8]{1,3,0,2:T(8,128)} %copy-done.11) | copy-start | bytes 1540
  474.0 14.2 %all-to-all-start.2 = ((f32[8,1,8192]{2,1,0:T(1,128)}), f32[8,1,8192]{2,1,0:T(1,128)S(1)}, u32[]{:S(2)}, u32[]{:S(2)}) async-start(f32[8,1,8192]{2,1,0:T(1,128)} %reshape.1563), calls=%async_computation.3 | async-start | bytes 524288 | tf_op jit(solution)/shard_map/all_to_all | solution.py:189
  479.9 15.5 %copy-start.9 = (f32[1,8,2,8]{1,3,0,2:T(8,128)}, f32[1,8,2,8]{1,3,0,2:T(8,128)S(1)}, u32[]{:S(2)}) copy-start(f32[1,8,2,8]{1,3,0,2:T(8,128)S(1)} %copy.335) | copy-start | bytes 1540
  498.7 17.9 %all-to-all-start.3 = ((f32[8,1,16384]{2,1,0:T(1,128)}), f32[8,1,16384]{2,1,0:T(1,128)S(1)}, u32[]{:S(2)}, u32[]{:S(2)}) async-start(f32[8,1,16384]{2,1,0:T(1,128)} %reshape.1565), calls=%async_computation.4 | async-start | bytes 1048576 | tf_op jit(solution)/shard_map/all_to_all | solution.py:207
  549.4 17.8 %all-to-all-start.5 = ((f32[8,1,16384]{2,1,0:T(1,128)}), f32[8,1,16384]{2,1,0:T(1,128)S(1)}, u32[]{:S(2)}, u32[]{:S(2)}) async-start(f32[8,1,16384]{2,1,0:T(1,128)} %reshape.1569), calls=%async_computation.6 | async-start | bytes 1048576 | tf_op jit(solution)/shard_map/all_to_all | solution.py:207
  553.0 24.3 %reduce-scatter.6.cloned.1.call-start = ((), (), s32[]{:S(2)}) async-start(), calls=%async_computation.11 | async-start | bytes 163840 | tf_op jit(solution)/shard_map/reduce_scatter | solution.py:226
  553.7 45.5 %reduce-scatter.8.cloned.1.call-start = ((), (), s32[]{:S(2)}) async-start(), calls=%async_computation.12 | async-start | bytes 163840 | tf_op jit(solution)/shard_map/reduce_scatter | solution.py:226
  574.2 26.5 %copy-start.4 = (f32[2,64,512]{2,1,0:T(8,128)}, f32[2,64,512]{2,1,0:T(8,128)S(1)}, u32[]{:S(2)}) copy-start(f32[2,64,512]{2,1,0:T(8,128)S(1)} %fusion.48) | copy-start | bytes 786436
  (30 other events, 121.3 us)
Sparse Core Ops, SparseCore 0:
  165.5 33.8 all-reduce.1
  202.4 20.4 reduce-scatter.3
  556.2 21.0 reduce-scatter.5
  579.6 19.6 reduce-scatter.7
